TPU v7x, 512 devices: a whole 4x8x8 slice. The times are simulated.
512 devices in a mesh: ep: 32 (over z, x), fsdp: 16 (over y, core).
Axes of the slice: x: 4, y: 8, z: 8, core: 2. Of those that a mesh axis runs over, the one named last changes fastest.
Arguments:
- train_down: float32 [64, 1408, 2048], P('ep', None, 'fsdp'), may hold values from -0.21875 to 0.21875
- other_down: float32 [64, 1408, 2048], P('ep', None, 'fsdp'), may hold values from -0.15625 to 0.15625
- router_weight: float32 [2048, 64], P('fsdp', 'ep'), may hold values from -0.125 to 0.125
- router_gain: float32 [2048], P('fsdp'), may hold values from 0.25 to 1.75
Outputs:
- ready_down: bfloat16 [64, 1408, 2048], P('ep')
- scale_down: float32 [64, 1408], P('ep')
- serve_router: bfloat16 [2048, 64], replicated
- latest_down: float32 [64, 1408, 2048], P('ep', None, 'fsdp')
All inputs are finite; a program needn't handle non-finite values.
Results may differ from a plain program's by a relative error of at most 0.001.
Values may be sent and summed in bfloat16 or wider, within the bound.
A program may use at most 128 MiB of HBM per device.

v0:
```python
import jax
import jax.numpy as jnp
from jax import lax
from jax.sharding import PartitionSpec as P


def from_everyone(x, axis):
    copies = jnp.broadcast_to(x, (lax.axis_size(axis), *x.shape))
    return lax.all_to_all(copies, axis, split_axis=0, concat_axis=0, tiled=True)


def taken_together(x, axis):
    return from_everyone(x, axis).sum(axis=0)


def laid_out(tiles, dim):
    shape = list(tiles.shape[1:])
    shape[dim] *= tiles.shape[0]
    return jnp.moveaxis(tiles, 0, dim).reshape(shape)


def gathered_copies(x, axis, dim):
    tiles = from_everyone(x, axis)
    return laid_out(tiles, dim)


def on_device(train_down, other_down, router_weight, router_gain):
    latest_down = 0.5 * other_down + 0.5 * train_down
    total_down = taken_together(jnp.sum(latest_down * latest_down, axis=2), "fsdp")
    scale_down = jnp.sqrt(total_down)
    narrow_down = (latest_down / jnp.expand_dims(scale_down, 2)).astype(jnp.bfloat16)
    ready_down = lax.all_gather(narrow_down, "fsdp", axis=2, tiled=True)
    part_router = (router_weight * router_gain[:, None]).astype(jnp.bfloat16)
    row_router = lax.all_gather(part_router, "fsdp", axis=0, tiled=True)
    serve_router = gathered_copies(row_router, "ep", 1)
    return (ready_down, scale_down, serve_router, latest_down)


def solution(mesh):
    placed = (P("ep", None, "fsdp"), P("ep", None, "fsdp"), P("fsdp", "ep"), P("fsdp"))
    return jax.shard_map(
        on_device,
        mesh=mesh,
        in_specs=placed,
        out_specs=(P("ep", None, None), P("ep", None), P(), P("ep", None, "fsdp")),
        check_vma=False,
    )
```

profile of v0, /device:TPU:1, one launch (start us, length us, event | category | flops | bytes accessed | tf_op | source)
XLA Modules:
  0.0 125.7 jit_solution(18168759618692292197)
XLA Ops:
  7.2 0.0 all-gather.2.cloned.1.call-start
  7.2 2.3 %multiply_reduce_fusion = (f32[2,1408]{1,0:T(2,128)S(1)}, f32[2,1408,128]{2,1,0:T(8,128)S(1)}) fusion(f32[2,1408,128]{2,1,0:T(8,128)} %param.5, f32[2,1408,128]{2,1,0:T(8,128)} %param.4), kind=kLoop, calls=%fused_computation.1 | loop fusion | flops 1438976 | bytes 4336640 | tf_op jit(solution)/shard_map/reduce_sum | solution.py:29
  9.5 0.0 copy-start
  9.5 19.2 %all_to_all.10 = f32[16,2,1408]{2,1,0:T(2,128)S(1)} all-to-all(f32[16,2,1408]{2,1,0:T(2,128)S(1)} %broadcast_in_dim.8), channel_id=1, replica_groups=mesh['ep'=32,'fsdp'=16] {'fsdp'}, dimensions={0} | all-to-all | bytes 360448 | tf_op jit(solution)/shard_map/all_to_all | solution.py:9
  28.7 0.1 reduce_sum.19
  28.8 0.0 copy-start.1
  28.8 0.0 copy-start.2
  28.8 0.0 copy-start.3
  28.8 1.3 %divide_convert_fusion = bf16[2,1408,128]{2,1,0:T(8,128)(2,1)} fusion(f32[2,1408,128]{2,1,0:T(8,128)S(1)} %get-tuple-element.13, f32[2,1408]{1,0:T(2,128)S(1)} %sqrt.7), kind=kLoop, calls=%fused_computation | loop fusion | flops 720896 | bytes 2173952 | tf_op jit(solution)/shard_map/convert_element_type | solution.py:31
  30.1 0.0 copy-done
  30.1 0.0 all-gather.2.cloned.1.call-update
  30.2 0.0 copy-done.1
  30.2 0.0 copy-done.2
  30.2 0.0 copy-done.3
  30.2 14.5 %all_gather.7 = bf16[2048,2]{0,1:T(2,128)(2,1)S(1)} all-gather(bf16[128,2]{0,1:T(2,128)(2,1)S(1)} %multiply_convert_fusion), channel_id=1, replica_groups=mesh['ep'=32,'fsdp'=16] {'fsdp'}, dimensions={0}, use_global_device_ids=true | all-gather | bytes 8704 | tf_op jit(solution)/shard_map/all_gather | solution.py:34
  44.7 0.1 broadcast_in_dim.9
  44.8 23.3 %all_to_all.11 = bf16[32,2048,2]{1,2,0:T(2,128)(2,1)S(1)} all-to-all(bf16[32,2048,2]{1,2,0:T(2,128)(2,1)S(1)} %broadcast_in_dim.9), channel_id=1, replica_groups=mesh['ep'=32,'fsdp'=16] {'ep'}, dimensions={0} | all-to-all | bytes 524288 | tf_op jit(solution)/shard_map/all_to_all | solution.py:9
  68.1 0.8 reshape.15
  68.9 39.8 %all-gather.2.cloned.1.call-done = bf16[2,1408,2048]{2,1,0:T(8,128)(2,1)} async-done(((bf16[2,1408,128]{2,1,0:T(8,128)(2,1)}), bf16[2,1408,2048]{2,1,0:T(8,128)(2,1)}) %all-gather.2.cloned.1.call-update) | async-done | bytes 11534352 | tf_op jit(solution)/shard_map/all_gather | solution.py:32
  108.7 10.1 %copy.11 = bf16[2,1408,2048]{2,1,0:T(8,128)(2,1)} copy(bf16[2,1408,2048]{2,1,0:T(8,128)(2,1)} %all-gather.2.cloned.1.call-done) | data formatting | bytes 23068672
  (3 shorter events, 0.1 us)
Async XLA Ops:
  7.2 101.6 %all-gather.2.cloned.1.call-start = ((), (), s32[]{:S(2)}) async-start(), calls=%async_computation.2 | async-start | bytes 12255232 | tf_op jit(solution)/shard_map/all_gather | solution.py:32
  9.5 20.7 %copy-start = (f32[2,1408,128]{2,1,0:T(8,128)}, f32[2,1408,128]{2,1,0:T(8,128)S(1)}, u32[]{:S(2)}) copy-start(f32[2,1408,128]{2,1,0:T(8,128)S(1)} %get-tuple-element.13) | copy-start | bytes 4325380
  28.8 1.4 %copy-start.1 = (f32[2,1408]{1,0:T(2,128)}, f32[2,1408]{1,0:T(2,128)S(1)}, u32[]{:S(2)}) copy-start(f32[2,1408]{1,0:T(2,128)S(1)} %sqrt.7) | copy-start | bytes 33796
  28.8 1.4 %copy-start.2 = (f32[128,2]{0,1:T(2,128)S(1)}, f32[128,2]{0,1:T(2,128)}, u32[]{:S(2)}) copy-start(f32[128,2]{0,1:T(2,128)} %param.6) | copy-start | bytes 3076
  28.8 1.4 %copy-start.3 = (f32[128]{0:T(128)S(1)}, f32[128]{0:T(128)}, u32[]{:S(2)}) copy-start(f32[128]{0:T(128)} %param.7) | copy-start | bytes 1540
Sparse Core Ops, SparseCore 0:
  30.3 78.3 all-gather.1
where the time goes:
time: 126 us
  blocking collectives  57 us (45%)
  waiting for transfers between devices  39.8 us (32%)
  between operations  14.1 us (11%)
  local copies, waits for them, and re-layouts  11.1 us (9%)
  other arithmetic  3.63 us (3%)
    all_to_all x2, blocking collectives, from_everyone(): return lax.all_to_all(copies, axis, split_axis=0, concat_axis=0, tiled=True)  42.5 us
    all_gather x1, waiting for transfers between devices, on_device(): ready_down = lax.all_gather(narrow_down, 'fsdp', axis=2, tiled=True)  39.8 us
    all_gather x1, blocking collectives, on_device(): row_router = lax.all_gather(part_router, 'fsdp', axis=0, tiled=True)  14.5 us
    unnamed x9, local copies, waits for them, and re-layouts  10.1 us
  transfers between devices with their start and end apart: 1, of which 1 were waited for; matrix products, arithmetic and copies ran while one was open for 1% of the time, Pallas kernels for 0%

commit v1 on v0

v1 whole, which is shorter than its diff:
```python
import functools

import jax
import jax.numpy as jnp
from jax import lax
from jax.experimental import pallas as pl
from jax.experimental.pallas import tpu as pltpu
from jax.sharding import PartitionSpec as P

MESH = pl.DeviceIdType.MESH
LANES = 128
CHUNKS = 8


def gather_kernel(
    ny, nz, nx, rows,
    train_ref, other_ref, weight_ref, gain_ref,
    land, scale_ref, router_ref, latest_ref,
    train_buf, other_buf, w_buf, g_buf, mine, sums, inverse, part, rland, load_sem, sum_send, sum_recv, ring_send, ring_recv,
    twin_send, twin_recv, rt_send, rt_recv, z_send, z_recv, x_send, x_recv,
):
    n = 2 * ny
    half = ny // 2
    total_rows = 2 * rows
    span = total_rows // CHUNKS
    groups = total_rows // 8
    vregs = (groups + LANES - 1) // LANES
    f_me = lax.axis_index("fsdp")
    e_me = lax.axis_index("ep")
    y, core = f_me // 2, lax.rem(f_me, 2)
    z, x = e_me // nx, lax.rem(e_me, nx)

    def column(y_index, core_index):
        return {"fsdp": y_index * 2 + core_index}

    right = column(lax.rem(y + 1, ny), core)
    left = column(lax.rem(y + ny - 1, ny), core)
    twin = column(y, 1 - core)
    peers = [lax.rem(f_me + d, n) for d in range(1, n)]
    z_peers = [lax.rem(z + d, nz) * nx + x for d in range(1, nz)]
    x_peers = [z * nx + lax.rem(x + d, nx) for d in range(1, nx)]

    def chunk(k):
        return pl.ds(pl.multiple_of(k * span, 16), span)

    small = (
        pltpu.make_async_copy(weight_ref, w_buf, load_sem.at[2 * CHUNKS]),
        pltpu.make_async_copy(gain_ref, g_buf, load_sem.at[2 * CHUNKS + 1]),
    )
    loads = []
    for k in range(CHUNKS):
        at = pl.ds(k * span, span)
        a = pltpu.make_async_copy(train_ref.at[at], train_buf.at[at], load_sem.at[2 * k])
        b = pltpu.make_async_copy(other_ref.at[at], other_buf.at[at], load_sem.at[2 * k + 1])
        a.start()
        b.start()
        loads.append((a, b))
    for c in small:
        c.start()

    barrier = pltpu.get_barrier_semaphore()
    for p in peers:
        pl.semaphore_signal(barrier, inc=1, device_id={"fsdp": p}, device_id_type=MESH)
    for p in z_peers + x_peers:
        pl.semaphore_signal(barrier, inc=1, device_id={"ep": p}, device_id_type=MESH)

    lane = lax.broadcasted_iota(jnp.int32, (8, LANES), 1)
    packed = None
    for g in range(groups):
        if g * 8 % span == 0:
            for c in loads[g * 8 // span]:
                c.wait()
        at = pl.ds(g * 8, 8)
        value = 0.5 * other_buf[at, :] + 0.5 * train_buf[at, :]
        latest_ref[at, :] = value
        total = jnp.sum(value * value, axis=1, keepdims=True)
        if g % LANES == 0:
            packed = jnp.ones((8, LANES), jnp.float32)
        packed = jnp.where(lane == g % LANES, total, packed)
        if g % LANES == LANES - 1 or g == groups - 1:
            mine[g // LANES] = packed
    for c in small:
        c.wait()
    part[...] = w_buf[...] * g_buf[...]

    pl.semaphore_wait(barrier, len(peers) + len(z_peers) + len(x_peers))

    def sum_copy(d, m):
        words = pl.ds(0, 1) if m == 0 else pl.ds(1, vregs - 1)
        return pltpu.make_async_remote_copy(
            mine.at[words], sums.at[f_me, words], sum_send.at[2 * d + m], sum_recv.at[2 * d + m],
            device_id={"fsdp": peers[d]}, device_id_type=MESH,
        )

    def router_copy(d):
        return pltpu.make_async_remote_copy(
            part, rland.at[z, x, f_me], rt_send.at[d], rt_recv.at[d],
            device_id={"fsdp": peers[d]}, device_id_type=MESH,
        )

    messages = 1 if vregs == 1 else 2
    far_first = sorted(range(n - 1), key=lambda d: -min(d + 1, n - 1 - d))
    for m in range(messages):
        for d in far_first:
            sum_copy(d, m).start()
    for d in far_first:
        router_copy(d).start()
    for m in range(vregs):
        sums[f_me, m] = mine[m]
    rland[z, x, f_me] = part[...]

    def ring_copy(way, hop, k, origin):
        block = land.at[2 * origin + core, chunk(k)]
        return pltpu.make_async_remote_copy(
            block, block, ring_send.at[way, hop - 1], ring_recv.at[way, hop - 1, k],
            device_id=right if way == 0 else left, device_id_type=MESH,
        )

    def twin_copy(hop, k, origin):
        block = land.at[2 * origin + core, chunk(k)]
        return pltpu.make_async_remote_copy(
            block, block, twin_send.at[hop], twin_recv.at[hop],
            device_id=twin, device_id_type=MESH,
        )

    done = 0
    for k in range(CHUNKS):
        need = ((k + 1) * span // 8 + LANES - 1) // LANES
        while done < need:
            m = 0 if done == 0 else 1
            if done < 2:
                for d in range(n - 1):
                    sum_copy(d, m).wait_recv()
            for v in range(done, 1 if m == 0 else vregs):
                total = sums[0, v]
                for s in range(1, n):
                    total = total + sums[s, v]
                scale = jnp.sqrt(total)
                mine_scale = scale
                inverse[0, v] = mine_scale
                inverse[1, v] = 1.0 / scale
            done = 1 if m == 0 else vregs
        for r in range(k * span // 16, (k + 1) * span // 16):
            both = []
            for g in (2 * r, 2 * r + 1):
                inv = inverse[1, g // LANES][:, g % LANES : g % LANES + 1]
                both.append(latest_ref[pl.ds(8 * g, 8), :] * jnp.broadcast_to(inv, (8, LANES)))
            land[f_me, pl.ds(16 * r, 16), :] = jnp.concatenate(both, axis=0).astype(jnp.bfloat16)
        ring_copy(0, 1, k, y).start()
        ring_copy(1, 1, k, y).start()
        twin_copy(0, k, y).start()

    for d in range(n - 1):
        router_copy(d).wait_recv()

    def z_copy(d):
        block = rland.at[z, x]
        return pltpu.make_async_remote_copy(
            block, block, z_send.at[d], z_recv.at[d], device_id={"ep": z_peers[d]}, device_id_type=MESH,
        )

    def x_copy(d):
        block = rland.at[:, x]
        return pltpu.make_async_remote_copy(
            block, block, x_send.at[d], x_recv.at[d], device_id={"ep": x_peers[d]}, device_id_type=MESH,
        )

    for d in range(nz - 1):
        z_copy(d).start()

    def origin_of(way, hop):
        return lax.rem(y + (ny - hop if way == 0 else hop), ny)

    def arrival(way, hop, k, onward):
        origin = origin_of(way, hop)
        ring_copy(way, hop, k, origin).wait_recv()
        if onward:
            ring_copy(way, hop + 1, k, origin).start()
        twin_copy(2 * hop + way if hop < half else 2 * half, k, origin).start()

    for hop in range(1, half):
        split = CHUNKS // 2
        last = hop == half - 1

        def first(k, c):
            arrival(0, hop, k, True)
            arrival(1, hop, k, not last)
            return c

        def second(k, c):
            arrival(0, hop, k, not last)
            arrival(1, hop, k, True)
            return c

        lax.fori_loop(0, split, first, 0)
        lax.fori_loop(split, CHUNKS, second, 0)
        if hop == 1:
            for d in range(nz - 1):
                z_copy(d).wait_recv()
            for d in range(nx - 1):
                x_copy(d).start()
            rows_at = lax.broadcasted_iota(jnp.int32, (LANES, LANES), 0)
            lanes_at = lax.broadcasted_iota(jnp.int32, (LANES, LANES), 1)
            for t in range(total_rows // LANES):
                tile = jnp.concatenate(
                    [
                        jnp.broadcast_to(inverse[0, g // LANES][:, g % LANES : g % LANES + 1], (8, LANES))
                        for g in range(16 * t, 16 * t + 16)
                    ],
                    axis=0,
                )
                line = jnp.sum(jnp.where(rows_at == lanes_at, tile, 0.0), axis=0, keepdims=True)
                e, at = divmod(t * LANES, rows)
                scale_ref[pl.ds(e, 1), pl.ds(at, LANES)] = line
    for d in range(nx - 1):
        x_copy(d).wait_recv()

    def lines(f, c):
        for q in range(nz * nx // 8):
            block = jnp.concatenate([rland[(8 * q + i) // nx, (8 * q + i) % nx, f] for i in range(8)], axis=0)
            router_ref[pl.ds(16 * q, 16), pl.ds(pl.multiple_of(f * LANES, LANES), LANES)] = block.astype(jnp.bfloat16)
        return c

    lax.fori_loop(0, n, lines, 0)

    def final(k, c):
        arrival(0, half, k, False)
        arrival(1, half, k + CHUNKS // 2, False)
        return c

    lax.fori_loop(0, CHUNKS // 2, final, 0)

    def whole(sem_send, sem_recv, part_rows):
        block = land.at[0, pl.ds(0, part_rows)]
        return pltpu.make_async_remote_copy(block, block, sem_send, sem_recv, device_id=twin, device_id_type=MESH)

    for hop in range(2 * half + 1):
        if hop == 1:
            continue
        whole(twin_send.at[hop], twin_recv.at[hop], total_rows).wait()
    for way in range(2):
        for hop in range(1, half + 1):
            part_rows = total_rows if hop < half else total_rows // 2
            whole(ring_send.at[way, hop - 1], twin_recv.at[0], part_rows).wait_send()
    for d in range(n - 1):
        for m in range(messages):
            sum_copy(d, m).wait_send()
        router_copy(d).wait_send()
    for d in range(nz - 1):
        z_copy(d).wait_send()
    for d in range(nx - 1):
        x_copy(d).wait_send()


def write_kernel(land, scale_in, router_in, latest_in, ready, scale, router, latest, sem):
    n = land.shape[0]
    copies = [
        pltpu.make_async_copy(land.at[f], ready.at[:, pl.ds(f * LANES, LANES)], sem.at[f]) for f in range(n)
    ]
    copies.append(pltpu.make_async_copy(scale_in, scale, sem.at[n]))
    copies.append(pltpu.make_async_copy(router_in, router, sem.at[n + 1]))
    copies.append(pltpu.make_async_copy(latest_in, latest, sem.at[n + 2]))
    for c in copies:
        c.start()
    for c in copies:
        c.wait()


def solution(mesh, nx=4):
    ep, n = mesh.shape["ep"], mesh.shape["fsdp"]
    ny, nz = n // 2, ep // nx

    def on_device(train_down, other_down, router_weight, router_gain):
        experts, rows, width = train_down.shape
        total_rows = experts * rows
        vregs = (total_rows // 8 + LANES - 1) // LANES
        f32, bf16 = jnp.float32, jnp.bfloat16
        half = ny // 2
        vmem = lambda shape, dtype: pltpu.VMEM(shape, dtype)
        dma = lambda *shape: pltpu.SemaphoreType.DMA(shape)
        anywhere = pl.BlockSpec(memory_space=pl.ANY)
        in_vmem = pl.BlockSpec(memory_space=pltpu.VMEM)
        results = pl.pallas_call(
            functools.partial(gather_kernel, ny, nz, nx, rows),
            out_shape=(
                pltpu.VMEM((n, total_rows, width), bf16),
                pltpu.VMEM((experts, rows), f32),
                pltpu.VMEM((ep * experts, n * width), bf16),
                pltpu.VMEM((total_rows, width), f32),
            ),
            in_specs=[pl.BlockSpec(memory_space=pltpu.HBM)] * 4,
            out_specs=(in_vmem,) * 4,
            scratch_shapes=[
                vmem((total_rows, width), f32),
                vmem((total_rows, width), f32),
                vmem((experts, width), f32),
                vmem((1, width), f32),
                vmem((vregs, 8, LANES), f32),
                vmem((n, vregs, 8, LANES), f32),
                vmem((2, vregs, 8, LANES), f32),
                vmem((experts, width), f32),
                vmem((nz, nx, n, experts, width), f32),
                dma(2 * CHUNKS + 2),
                dma(2 * (n - 1)),
                dma(2 * (n - 1)),
                dma(2, half),
                dma(2, half, CHUNKS),
                dma(2 * half + 1),
                dma(2 * half + 1),
                dma(n - 1),
                dma(n - 1),
                dma(nz),
                dma(nz),
                dma(nx),
                dma(nx),
            ],
            compiler_params=pltpu.CompilerParams(
                collective_id=0, has_side_effects=True, vmem_limit_bytes=24 * 1024 * 1024
            ),
            name="gather",
        )(
            *(
                pltpu.with_memory_space_constraint(a, pltpu.HBM)
                for a in (
                    train_down.reshape(total_rows, width),
                    other_down.reshape(total_rows, width),
                    router_weight.T,
                    router_gain.reshape(1, width),
                )
            )
        )
        held = [pltpu.with_memory_space_constraint(r, pltpu.VMEM) for r in results]
        ready, scale, router, latest = pl.pallas_call(
            write_kernel,
            out_shape=(
                jax.ShapeDtypeStruct((total_rows, n * width), bf16),
                jax.ShapeDtypeStruct((experts, rows), f32),
                jax.ShapeDtypeStruct((ep * experts, n * width), bf16),
                jax.ShapeDtypeStruct((total_rows, width), f32),
            ),
            in_specs=[in_vmem] * 4,
            out_specs=(anywhere,) * 4,
            scratch_shapes=[dma(n + 3)],
            compiler_params=pltpu.CompilerParams(vmem_limit_bytes=1024 * 1024),
            name="write",
        )(*held)
        return (
            ready.reshape(experts, rows, n * width),
            scale,
            router.T,
            latest.reshape(experts, rows, width),
        )

    placed = (P("ep", None, "fsdp"), P("ep", None, "fsdp"), P("fsdp", "ep"), P("fsdp"))
    return jax.shard_map(
        on_device,
        mesh=mesh,
        in_specs=placed,
        out_specs=(P("ep", None, None), P("ep", None), P(), P("ep", None, "fsdp")),
        check_vma=False,
    )
```

time: 126 us -> 84.2 us (0.67)
  Pallas kernels: 0 us -> 83.4 us
  blocking collectives: 57 us -> 0 us
  waiting for transfers between devices: 39.8 us -> 0 us
  between operations: 14.1 us -> 0.64 us
  local copies, waits for them, and re-layouts: 11.1 us -> 0 us
  other arithmetic: 3.63 us -> 0 us
    pallas_call x0 -> x2, Pallas kernels: none -> 83.4 us  [the longest x1 78.4 us: on_device(): pl.pallas_call(functools.partial(gather_kernel, ny, nz, nx, rows), out_sh...]
    all_to_all x2 -> x0, blocking collectives: 42.5 us -> none  [from_everyone(): return lax.all_to_all(copies, axis, split_axis=0, concat_axis=0, tiled=True)]
    all_gather x1 -> x0, waiting for transfers between devices: 39.8 us -> none  [on_device(): ready_down = lax.all_gather(narrow_down, 'fsdp', axis=2, tiled=True)]
    all_gather x1 -> x0, blocking collectives: 14.5 us -> none  [on_device(): row_router = lax.all_gather(part_router, 'fsdp', axis=0, tiled=True)]
    unnamed x9 -> x0, local copies, waits for them, and re-layouts: 10.1 us -> none
    reduce_sum x2 -> x0, other arithmetic: 2.32 us -> none  [the longest x1 2.25 us: on_device(): jnp.sum(latest_down * latest_down, axis=2)]
    convert_element_type x2 -> x0, other arithmetic: 1.31 us -> none  [the longest x1 1.3 us: on_device(): (latest_down / jnp.expand_dims(scale_down, 2)).astype(jnp.bfloat16)]
  transfers between devices with their start and end apart: 1 -> 0, of which waited for: 1 -> 0; matrix products, arithmetic and copies ran while one was open for 1% -> 0% of each run, Pallas kernels for 0% -> 0%
where the time goes in v1:
time: 84.2 us; the launch traced here: 84 us
  Pallas kernels  83.4 us (99%)
    pallas_call x1, Pallas kernels, on_device(): pl.pallas_call(functools.partial(gather_kernel, ny, nz, nx, rows), out_sh...  78.4 us
    pallas_call x1, Pallas kernels, on_device(): pl.pallas_call(write_kernel, out_shape=(jax.ShapeDtypeStruct((total_rows,...  4.94 us

profile of v1, /device:TPU:1, one launch (start us, length us, event | category | flops | bytes accessed | tf_op | source)
XLA Modules:
  0.0 84.0 jit_solution(27923156467998340)
XLA Ops:
  0.6 78.4 %gather.1 = (bf16[16,2816,128]{2,1,0:T(8,128)(2,1)S(1)}, f32[2,1408]{1,0:T(2,128)S(1)}, bf16[64,2048]{1,0:T(8,128)(2,1)S(1)}, f32[2816,128]{1,0:T(8,128)S(1)}) custom-call(f32[2816,128]{1,0:T(8,128)} %bitcast.7, f32[2816,128]{1,0:T(8,128)} %bitcast.8, f32[2,128]{1,0:T(2,128)} %bitcast.9, f32[1,128]{1,0:T(1,128)} %bitcast.10), custom_call_target="tpu_custom_call" | custom-call | tf_op jit(solution)/shard_map/gather/pallas_call | solution.py:283
  79.1 4.9 %write.1 = (bf16[2816,2048]{1,0:T(8,128)(2,1)}, f32[2,1408]{1,0:T(2,128)}, bf16[64,2048]{1,0:T(8,128)(2,1)}, f32[2816,128]{1,0:T(8,128)}) custom-call(bf16[16,2816,128]{2,1,0:T(8,128)(2,1)S(1)} %get-tuple-element.12.land, f32[2,1408]{1,0:T(2,128)S(1)} %get-tuple-element.13.scale_in, bf16[64,2048]{1,0:T(8,128)(2,1)S(1)} %get-tuple-element.14.router_in, ...), custom_call_target="tpu_custom_call" | custom-call | tf_op jit(solution)/shard_map/write/pallas_call | solution.py:333

commit v2 on v1

v2 whole, which is shorter than its diff:
```python
import functools

import jax
import jax.numpy as jnp
from jax import lax
from jax.experimental import pallas as pl
from jax.experimental.pallas import tpu as pltpu
from jax.sharding import PartitionSpec as P

MESH = pl.DeviceIdType.MESH
LANES = 128
CHUNKS = 16
EARLY = 6
RANGE = 240.0
TINY = 1e-36
TURNS = (3, 6, 9, 12, 13, 19, 26)
LN2 = 0.6931471805599453


def gather_kernel(
    ny, nz, nx, rows,
    train_ref, other_ref, weight_ref, gain_ref,
    land, scale_ref, router_ref, latest_ref,
    train_buf, other_buf, w_buf, g_buf, code, sums, inverse, factor, rland, load_sem, sum_send, sum_recv, ring_send, ring_recv,
    twin_send, twin_recv, tsum_send, tsum_recv, tcode_send, tcode_recv, z_send, z_recv, x_send, x_recv,
):
    n = 2 * ny
    half = ny // 2
    total_rows = 2 * rows
    span = total_rows // CHUNKS
    early_rows = EARLY * span
    groups = total_rows // 8
    vregs = (groups + LANES - 1) // LANES
    f_me = lax.axis_index("fsdp")
    e_me = lax.axis_index("ep")
    y, core = f_me // 2, lax.rem(f_me, 2)
    z, x = e_me // nx, lax.rem(e_me, nx)

    def column(y_index, core_index):
        return {"fsdp": y_index * 2 + core_index}

    right = column(lax.rem(y + 1, ny), core)
    left = column(lax.rem(y + ny - 1, ny), core)
    twin = column(y, 1 - core)
    z_next = {"ep": lax.rem(z + 1, nz) * nx + x}
    z_last = {"ep": lax.rem(z + nz - 1, nz) * nx + x}
    x_next = {"ep": z * nx + lax.rem(x + 1, nx)}
    x_last = {"ep": z * nx + lax.rem(x + nx - 1, nx)}
    neighbours = [right, left, twin] + ([z_next, z_last] if nz > 1 else []) + ([x_next, x_last] if nx > 1 else [])

    small = (
        pltpu.make_async_copy(weight_ref, w_buf, load_sem.at[2 * CHUNKS]),
        pltpu.make_async_copy(gain_ref, g_buf, load_sem.at[2 * CHUNKS + 1]),
    )
    loads = []
    for k in range(CHUNKS):
        at = pl.ds(k * span, span)
        a = pltpu.make_async_copy(train_ref.at[at], train_buf.at[at], load_sem.at[2 * k])
        b = pltpu.make_async_copy(other_ref.at[at], other_buf.at[at], load_sem.at[2 * k + 1])
        a.start()
        b.start()
        loads.append((a, b))
        if k == 0:
            for c in small:
                c.start()

    barrier = pltpu.get_barrier_semaphore()
    for p in neighbours:
        pl.semaphore_signal(barrier, inc=1, device_id=p, device_id_type=MESH)

    def origin_of(way, hop):
        return lax.rem(y + (ny - hop if way == 0 else hop), ny)

    def apart(way, hop):
        return 0 if hop == 0 else (ny - hop if way == 0 else hop)

    def piece(k, origin, early):
        buf = code if early else land
        return buf.at[2 * origin + core, pl.ds(pl.multiple_of(k * span, 16), span)]

    def ring_copy(way, hop, k, early):
        block = piece(k, origin_of(way, hop - 1), early)
        return pltpu.make_async_remote_copy(
            block, block, ring_send.at[way, hop - 1], ring_recv.at[way, hop - 1, k],
            device_id=right if way == 0 else left, device_id_type=MESH,
        )

    def ring_wait(way, hop, k, early):
        block = piece(k, origin_of(way, hop), early)
        pltpu.make_async_remote_copy(
            block, block, ring_send.at[way, hop - 1], ring_recv.at[way, hop - 1, k],
            device_id=right if way == 0 else left, device_id_type=MESH,
        ).wait_recv()

    def twin_copy(way, hop, k, early):
        block = piece(k, origin_of(way, hop), early)
        d = apart(way, hop)
        return pltpu.make_async_remote_copy(
            block, block, (tcode_send if early else twin_send).at[d], (tcode_recv if early else twin_recv).at[d],
            device_id=twin, device_id_type=MESH,
        )

    def launch(k, early):
        ring_copy(0, 1, k, early).start()
        ring_copy(1, 1, k, early).start()
        twin_copy(0, 0, k, early).start()

    def arrival(way, hop, k, early, onward):
        ring_wait(way, hop, k, early)
        if onward:
            ring_copy(way, hop + 1, k, early).start()
        twin_copy(way, hop, k, early).start()

    def sum_copy(way, hop):
        block = sums.at[2 * origin_of(way, hop - 1) + core]
        return pltpu.make_async_remote_copy(
            block, block, sum_send.at[way, hop - 1], sum_recv.at[way, hop - 1],
            device_id=right if way == 0 else left, device_id_type=MESH,
        )

    def sum_wait(way, hop):
        block = sums.at[2 * origin_of(way, hop) + core]
        pltpu.make_async_remote_copy(
            block, block, sum_send.at[way, hop - 1], sum_recv.at[way, hop - 1],
            device_id=right if way == 0 else left, device_id_type=MESH,
        ).wait_recv()

    def sum_twin(d, whose):
        block = sums.at[2 * lax.rem(y + d, ny) + whose]
        return pltpu.make_async_remote_copy(
            block, block, tsum_send.at[d], tsum_recv.at[d], device_id=twin, device_id_type=MESH,
        )

    lane = lax.broadcasted_iota(jnp.int32, (8, LANES), 1)
    ones = jnp.ones((8, LANES), jnp.float32)
    words = [ones]

    def sweep(k):
        for c in loads[k]:
            c.wait()
        both = []
        for g in range(k * span // 8, (k + 1) * span // 8):
            at = pl.ds(g * 8, 8)
            value = 0.5 * other_buf[at, :] + 0.5 * train_buf[at, :]
            latest_ref[at, :] = value
            total = jnp.sum(value * value, axis=1, keepdims=True)
            words[0] = jnp.where(lane == g % LANES, total, words[0])
            if g % LANES == LANES - 1 or g == groups - 1:
                sums[f_me, g // LANES] = words[0]
                words[0] = ones
            if k < EARLY:
                reach = RANGE * lax.rsqrt(jnp.maximum(jnp.broadcast_to(total, (8, LANES)), TINY))
                size = jnp.exp(LN2 * (jnp.abs(value) * reach - RANGE / 2))
                both.append(jnp.where(value < 0, -size, size))
                if len(both) == 2:
                    code[f_me, pl.ds((g - 1) * 8, 16), :] = jnp.concatenate(both, axis=0).astype(jnp.bfloat16)
                    both = []

    sweep(0)
    pl.semaphore_wait(barrier, len(neighbours))
    launch(0, True)
    sweep(1)
    launch(1, True)
    for k in range(2, CHUNKS):
        sweep(k)
        if k == 2:
            for c in small:
                c.wait()
            sums[f_me, vregs, pl.ds(0, 2), :] = w_buf[...] * g_buf[...]
    sum_copy(0, 1).start()
    sum_copy(1, 1).start()
    sum_twin(0, core).start()
    for k in range(2, min(4, EARLY)):
        launch(k, True)

    mid = EARLY // 2

    def early_step(hop, k):
        last = hop == half - 1
        arrival(0, hop, k, True, not last or k < mid)
        arrival(1, hop, k, True, not last or k >= mid)

    waiting = [(0, k) for k in range(4, EARLY)] + [(hop, k) for hop in range(1, half) for k in range(EARLY)]

    ahead = []

    def early_some(count):
        ahead.extend(waiting[:count])
        for hop, k in waiting[:count]:
            if hop == 0:
                launch(k, True)
            else:
                early_step(hop, k)
        del waiting[:count]

    for hop in range(1, half + 1):
        sum_wait(0, hop)
        if hop < half:
            sum_copy(0, hop + 1).start()
            sum_wait(1, hop)
            if hop < half - 1:
                sum_copy(1, hop + 1).start()
            sum_twin(apart(1, hop), core).start()
        sum_twin(apart(0, hop), core).start()
        early_some(3)
    for d in range(ny):
        sum_twin(d, 1 - core).wait_recv()

    for v in range(vregs):
        total = sums[0, v]
        for s in range(1, n):
            total = total + sums[s, v]
        scale = jnp.sqrt(total)
        inverse[0, v] = scale
        inverse[1, v] = 1.0 / scale

    def scaled(r):
        both = []
        for g in (2 * r, 2 * r + 1):
            inv = inverse[1, g // LANES][:, g % LANES : g % LANES + 1]
            both.append(latest_ref[pl.ds(8 * g, 8), :] * jnp.broadcast_to(inv, (8, LANES)))
        land[f_me, pl.ds(16 * r, 16), :] = jnp.concatenate(both, axis=0).astype(jnp.bfloat16)

    for k in range(EARLY, CHUNKS):
        for r in range(k * span // 16, (k + 1) * span // 16):
            scaled(r)
        launch(k, False)
    sent = {(hop + 1, k) for hop, k in ahead}
    first = [(hop, k) for hop, k in waiting if hop == 1 or (hop, k) in sent]
    second = [step for step in waiting if step not in first]
    for hop, k in first:
        early_step(hop, k)

    for f in range(n):
        rland[z, x, f] = sums[f, vregs, pl.ds(0, 2), :]

    def z_copy(way, step, where):
        block = rland.at[where, x]
        return pltpu.make_async_remote_copy(
            block, block, z_send.at[way, step], z_recv.at[way, step],
            device_id=z_last if way else z_next, device_id_type=MESH,
        )

    def x_copy(way, step, where):
        block = rland.at[:, where]
        return pltpu.make_async_remote_copy(
            block, block, x_send.at[way, step], x_recv.at[way, step],
            device_id=x_last if way else x_next, device_id_type=MESH,
        )

    def round_step(copy, size, me, step):
        for way, hops in enumerate((size // 2, size - 1 - size // 2)):
            where = lax.rem(me + size + (step if way else -step), size)
            if 1 <= step <= hops:
                copy(way, step - 1, where).wait_recv()
            if step < hops:
                copy(way, step, where).start()

    tasks = [functools.partial(round_step, z_copy, nz, z, step) for step in range(nz // 2 + 1)]
    tasks += [functools.partial(round_step, x_copy, nx, x, step) for step in range(nx // 2 + 1)]

    for s in range(n):
        for v in range(factor.shape[1]):
            factor[s, v] = jnp.sqrt(jnp.maximum(sums[s, v], TINY)) * inverse[1, v] * (1.0 / RANGE)
    for r in range(early_rows // 16):
        scaled(r)
    tasks.pop(0)()

    def decode(i):
        far = ((i >= ny - 2) & (i < 2 * ny - 3)) | (i == 2 * ny - 2)
        near = jnp.where(far, i - (ny - 2), i + 1)
        offset = jnp.where(i >= 2 * ny - 3, half, near + jnp.where(near >= half, 1, 0))
        slot = 2 * lax.rem(y + offset, ny) + jnp.where(far, 1 - core, core)

        @pl.when(far)
        def _():
            block = code.at[slot]
            pltpu.make_async_remote_copy(
                block, block, tcode_send.at[offset], tcode_recv.at[offset], device_id=twin, device_id_type=MESH,
            ).wait_recv()

        by = [factor[slot, v] for v in range(factor.shape[1])]
        for r in range(early_rows // 16):
            held = code[slot, pl.ds(16 * r, 16), :].astype(jnp.float32)
            size = jnp.log(jnp.abs(held)) * (1.0 / LN2) + RANGE / 2
            signed = jnp.where(held < 0, -size, size)
            part = jnp.concatenate(
                [
                    jnp.broadcast_to(by[g // LANES][:, g % LANES : g % LANES + 1], (8, LANES))
                    for g in (2 * r, 2 * r + 1)
                ],
                axis=0,
            )
            land[slot, pl.ds(16 * r, 16), :] = (signed * part).astype(jnp.bfloat16)

    late = CHUNKS - EARLY
    turn = EARLY + late // 2
    codes = n - 1

    def pair(hop, k, extra):
        if hop < half - 1:
            arrival(0, hop, k, False, True)
            arrival(1, hop, k, False, True)
        else:
            for way in range(2):
                ring_wait(way, hop, k, False)
                twin_copy(way, hop, k, False).start()

            @pl.when(k < turn)
            def _():
                ring_copy(0, hop + 1, k, False).start()

            @pl.when(k >= turn)
            def _():
                ring_copy(1, hop + 1, k, False).start()
        extra(k)

    def decode_step(base):
        def run(k):
            i = base + k - EARLY

            @pl.when(i < codes)
            def _():
                decode(i)

        return run

    due = {}
    for i, task in enumerate(tasks):
        if half == 1 or i >= len(TURNS):
            due.setdefault((half - 1, CHUNKS - 1), []).append(task)
        else:
            hop, k = divmod(TURNS[i], late)
            due.setdefault((min(hop + 1, half - 1), k + EARLY), []).append(task)

    for hop in range(1, half):

        def extra(k, hop=hop):
            for (at_hop, at), todo in due.items():
                if at_hop == hop:

                    @pl.when(k == at)
                    def _(todo=todo):
                        for task in todo:
                            task()

            if hop > 1:
                decode_step(late * (hop - 2))(k)

        def body(k, c, hop=hop, extra=extra):
            pair(hop, k, extra)
            return c

        lax.fori_loop(EARLY, CHUNKS, body, 0)
        if hop == 1:
            for early_hop, k in second:
                early_step(early_hop, k)
        if hop == min(2, half - 1):
            for k in range(mid):
                arrival(0, half, k, True, False)
                arrival(1, half, k + mid, True, False)
        if hop == 1:
            rows_at = lax.broadcasted_iota(jnp.int32, (LANES, LANES), 0)
            lanes_at = lax.broadcasted_iota(jnp.int32, (LANES, LANES), 1)
            for t in range(total_rows // LANES):
                tile = jnp.concatenate(
                    [
                        jnp.broadcast_to(inverse[0, g // LANES][:, g % LANES : g % LANES + 1], (8, LANES))
                        for g in range(16 * t, 16 * t + 16)
                    ],
                    axis=0,
                )
                line = jnp.sum(jnp.where(rows_at == lanes_at, tile, 0.0), axis=0, keepdims=True)
                e, at = divmod(t * LANES, rows)
                scale_ref[pl.ds(e, 1), pl.ds(at, LANES)] = line
    for i in range(late * (half - 2), codes):
        decode(jnp.int32(i))

    def lines(f, c):
        for q in range(nz * nx // 8):
            block = jnp.concatenate([rland[(8 * q + i) // nx, (8 * q + i) % nx, f] for i in range(8)], axis=0)
            router_ref[pl.ds(16 * q, 16), pl.ds(pl.multiple_of(f * LANES, LANES), LANES)] = block.astype(jnp.bfloat16)
        return c

    lax.fori_loop(0, n, lines, 0)

    def final(k, c):
        arrival(0, half, k, False, False)
        arrival(1, half, k + late // 2, False, False)
        return c

    lax.fori_loop(EARLY, turn, final, 0)

    def whole(buf, send, recv, part_rows):
        block = buf.at[0, pl.ds(0, part_rows)]
        return pltpu.make_async_remote_copy(block, block, send, recv, device_id=twin, device_id_type=MESH)

    for way in range(2):
        for hop in range(1, half + 1):
            part_rows = total_rows if hop < half else total_rows // 2
            whole(land, ring_send.at[way, hop - 1], twin_recv.at[0], part_rows).wait_send()
    for way in range(2):
        for hop in range(1, half + 1 - way):
            sum_copy(way, hop).wait_send()
    for d in range(ny):
        sum_twin(d, core).wait_send()
        whole(code, tcode_send.at[d], tcode_recv.at[d], early_rows).wait_send()
    for copy, size, me in ((z_copy, nz, z), (x_copy, nx, x)):
        for way, hops in enumerate((size // 2, size - 1 - size // 2)):
            for step in range(hops):
                copy(way, step, me).wait_send()
    for d in range(ny):
        whole(land, twin_send.at[d], twin_recv.at[d], total_rows - early_rows).wait()


def write_kernel(land, scale_in, router_in, latest_in, ready, scale, router, latest, sem):
    n = land.shape[0]
    copies = [
        pltpu.make_async_copy(land.at[f], ready.at[:, pl.ds(f * LANES, LANES)], sem.at[f]) for f in range(n)
    ]
    copies.append(pltpu.make_async_copy(scale_in, scale, sem.at[n]))
    copies.append(pltpu.make_async_copy(router_in, router, sem.at[n + 1]))
    copies.append(pltpu.make_async_copy(latest_in, latest, sem.at[n + 2]))
    for c in copies:
        c.start()
    for c in copies:
        c.wait()


def solution(mesh, nx=4):
    ep, n = mesh.shape["ep"], mesh.shape["fsdp"]
    ny, nz = n // 2, ep // nx

    def on_device(train_down, other_down, router_weight, router_gain):
        experts, rows, width = train_down.shape
        total_rows = experts * rows
        vregs = (total_rows // 8 + LANES - 1) // LANES
        f32, bf16 = jnp.float32, jnp.bfloat16
        half = ny // 2
        vmem = lambda shape, dtype: pltpu.VMEM(shape, dtype)
        dma = lambda *shape: pltpu.SemaphoreType.DMA(shape)
        anywhere = pl.BlockSpec(memory_space=pl.ANY)
        in_vmem = pl.BlockSpec(memory_space=pltpu.VMEM)
        results = pl.pallas_call(
            functools.partial(gather_kernel, ny, nz, nx, rows),
            out_shape=(
                pltpu.VMEM((n, total_rows, width), bf16),
                pltpu.VMEM((experts, rows), f32),
                pltpu.VMEM((ep * experts, n * width), bf16),
                pltpu.VMEM((total_rows, width), f32),
            ),
            in_specs=[pl.BlockSpec(memory_space=pltpu.HBM)] * 4,
            out_specs=(in_vmem,) * 4,
            scratch_shapes=[
                vmem((total_rows, width), f32),
                vmem((total_rows, width), f32),
                vmem((experts, width), f32),
                vmem((1, width), f32),
                vmem((n, total_rows * EARLY // CHUNKS, width), bf16),
                vmem((n, vregs + 1, 8, LANES), f32),
                vmem((2, vregs, 8, LANES), f32),
                vmem((n, -(-total_rows * EARLY // CHUNKS // (8 * LANES)), 8, LANES), f32),
                vmem((nz, nx, n, experts, width), f32),
                dma(2 * CHUNKS + 2),
                dma(2, half),
                dma(2, half),
                dma(2, half),
                dma(2, half, CHUNKS),
                dma(ny),
                dma(ny),
                dma(ny),
                dma(ny),
                dma(ny),
                dma(ny),
                dma(2, nz // 2 + 1),
                dma(2, nz // 2 + 1),
                dma(2, nx // 2 + 1),
                dma(2, nx // 2 + 1),
            ],
            compiler_params=pltpu.CompilerParams(
                collective_id=0, has_side_effects=True, vmem_limit_bytes=24 * 1024 * 1024
            ),
            name="gather",
        )(
            *(
                pltpu.with_memory_space_constraint(a, pltpu.HBM)
                for a in (
                    train_down.reshape(total_rows, width),
                    other_down.reshape(total_rows, width),
                    router_weight.T,
                    router_gain.reshape(1, width),
                )
            )
        )
        held = [pltpu.with_memory_space_constraint(r, pltpu.VMEM) for r in results]
        ready, scale, router, latest = pl.pallas_call(
            write_kernel,
            out_shape=(
                jax.ShapeDtypeStruct((total_rows, n * width), bf16),
                jax.ShapeDtypeStruct((experts, rows), f32),
                jax.ShapeDtypeStruct((ep * experts, n * width), bf16),
                jax.ShapeDtypeStruct((total_rows, width), f32),
            ),
            in_specs=[in_vmem] * 4,
            out_specs=(anywhere,) * 4,
            scratch_shapes=[dma(n + 3)],
            compiler_params=pltpu.CompilerParams(vmem_limit_bytes=1024 * 1024),
            name="write",
        )(*held)
        return (
            ready.reshape(experts, rows, n * width),
            scale,
            router.T,
            latest.reshape(experts, rows, width),
        )

    placed = (P("ep", None, "fsdp"), P("ep", None, "fsdp"), P("fsdp", "ep"), P("fsdp"))
    return jax.shard_map(
        on_device,
        mesh=mesh,
        in_specs=placed,
        out_specs=(P("ep", None, None), P("ep", None), P(), P("ep", None, "fsdp")),
        check_vma=False,
    )
```

time: 84.2 us -> 79.8 us (0.948)
  Pallas kernels: 83.4 us -> 79 us
    pallas_call x1, Pallas kernels: 78.4 us -> 74.1 us  [on_device(): pl.pallas_call(functools.partial(gather_kernel, ny, nz, nx, rows), out_sh...]
where the time goes in v2:
time: 79.8 us; the launch traced here: 79.7 us
  Pallas kernels  79 us (99%)
    pallas_call x1, Pallas kernels, on_device(): pl.pallas_call(functools.partial(gather_kernel, ny, nz, nx, rows), out_sh...  74.1 us
    pallas_call x1, Pallas kernels, on_device(): pl.pallas_call(write_kernel, out_shape=(jax.ShapeDtypeStruct((total_rows,...  4.94 us

profile of v2, /device:TPU:1, one launch (start us, length us, event | category | flops | bytes accessed | tf_op | source)
XLA Modules:
  0.0 79.7 jit_solution(9563077386359637692)
XLA Ops:
  0.6 74.1 %gather.1 = (bf16[16,2816,128]{2,1,0:T(8,128)(2,1)S(1)}, f32[2,1408]{1,0:T(2,128)S(1)}, bf16[64,2048]{1,0:T(8,128)(2,1)S(1)}, f32[2816,128]{1,0:T(8,128)S(1)}) custom-call(f32[2816,128]{1,0:T(8,128)} %bitcast.7, f32[2816,128]{1,0:T(8,128)} %bitcast.8, f32[2,128]{1,0:T(2,128)} %bitcast.9, f32[1,128]{1,0:T(1,128)} %bitcast.10), custom_call_target="tpu_custom_call" | custom-call | tf_op jit(solution)/shard_map/gather/pallas_call | solution.py:444
  74.7 4.9 %write.1 = (bf16[2816,2048]{1,0:T(8,128)(2,1)}, f32[2,1408]{1,0:T(2,128)}, bf16[64,2048]{1,0:T(8,128)(2,1)}, f32[2816,128]{1,0:T(8,128)}) custom-call(bf16[16,2816,128]{2,1,0:T(8,128)(2,1)S(1)} %get-tuple-element.12.land, f32[2,1408]{1,0:T(2,128)S(1)} %get-tuple-element.13.scale_in, bf16[64,2048]{1,0:T(8,128)(2,1)S(1)} %get-tuple-element.14.router_in, ...), custom_call_target="tpu_custom_call" | custom-call | tf_op jit(solution)/shard_map/write/pallas_call | solution.py:496

commit v3 on v2

--- a/solution.py
+++ b/solution.py
@@ -13,7 +13,7 @@
 EARLY = 6
 RANGE = 240.0
 TINY = 1e-36
-TURNS = (3, 6, 9, 12, 13, 19, 26)
+TURNS = (6, 9, 12, 15, 16, 22, 28)
 LN2 = 0.6931471805599453
 
 
@@ -22,7 +22,7 @@
     train_ref, other_ref, weight_ref, gain_ref,
     land, scale_ref, router_ref, latest_ref,
     train_buf, other_buf, w_buf, g_buf, code, sums, inverse, factor, rland, load_sem, sum_send, sum_recv, ring_send, ring_recv,
-    twin_send, twin_recv, tsum_send, tsum_recv, tcode_send, tcode_recv, z_send, z_recv, x_send, x_recv,
+    twin_send, twin_recv, tsum_send, tsum_recv, tcode_send, tcode_recv, z_send, z_recv, x_send, x_recv, here_sem,
 ):
     n = 2 * ny
     half = ny // 2
@@ -46,13 +46,19 @@
     z_last = {"ep": lax.rem(z + nz - 1, nz) * nx + x}
     x_next = {"ep": z * nx + lax.rem(x + 1, nx)}
     x_last = {"ep": z * nx + lax.rem(x + nx - 1, nx)}
-    neighbours = [right, left, twin] + ([z_next, z_last] if nz > 1 else []) + ([x_next, x_last] if nx > 1 else [])
+    line = [right, left, twin]
+    across = []
+    if nz > 1:
+        across += [(z_next, lax.rem(z + 1, nz), z, 0), (z_last, lax.rem(z + nz - 1, nz), z, 0)]
+    if nx > 1:
+        across += [(x_next, lax.rem(x + 1, nx), x, 1), (x_last, lax.rem(x + nx - 1, nx), x, 1)]
 
     small = (
         pltpu.make_async_copy(weight_ref, w_buf, load_sem.at[2 * CHUNKS]),
         pltpu.make_async_copy(gain_ref, g_buf, load_sem.at[2 * CHUNKS + 1]),
     )
     loads = []
+    barrier = pltpu.get_barrier_semaphore()
     for k in range(CHUNKS):
         at = pl.ds(k * span, span)
         a = pltpu.make_async_copy(train_ref.at[at], train_buf.at[at], load_sem.at[2 * k])
@@ -61,12 +67,16 @@
         b.start()
         loads.append((a, b))
         if k == 0:
-            for c in small:
-                c.start()
-
-    barrier = pltpu.get_barrier_semaphore()
-    for p in neighbours:
-        pl.semaphore_signal(barrier, inc=1, device_id=p, device_id_type=MESH)
+            for p in line:
+                pl.semaphore_signal(barrier, inc=1, device_id=p, device_id_type=MESH)
+    for c in small:
+        c.start()
+    for p, there, here, _ in across:
+
+        @pl.when(there > here)
+        def _(p=p):
+            pl.semaphore_signal(barrier, inc=1, device_id=p, device_id_type=MESH)
+
 
     def origin_of(way, hop):
         return lax.rem(y + (ny - hop if way == 0 else hop), ny)
@@ -157,8 +167,15 @@
                     both = []
 
     sweep(0)
-    pl.semaphore_wait(barrier, len(neighbours))
+    lower = [jnp.where(there < here, 1, 0) for _, there, here, _ in across]
+    pl.semaphore_wait(barrier, sum(lower, len(line)))
     launch(0, True)
+    for p, there, here, axis in across:
+
+        @pl.when(there < here)
+        def _(p=p, axis=axis):
+            pl.semaphore_signal(here_sem.at[axis], inc=1, device_id=p, device_id_type=MESH)
+
     sweep(1)
     launch(1, True)
     for k in range(2, CHUNKS):
@@ -264,6 +281,14 @@
             factor[s, v] = jnp.sqrt(jnp.maximum(sums[s, v], TINY)) * inverse[1, v] * (1.0 / RANGE)
     for r in range(early_rows // 16):
         scaled(r)
+    for axis in range(2):
+        higher = [jnp.where(there > here, 1, 0) for _, there, here, a in across if a == axis]
+        if higher:
+
+            @pl.when(sum(higher) > 0)
+            def _(axis=axis, count=sum(higher)):
+                pl.semaphore_wait(here_sem.at[axis], count)
+
     tasks.pop(0)()
 
     def decode(i):
@@ -476,6 +501,7 @@
                 dma(2, nz // 2 + 1),
                 dma(2, nx // 2 + 1),
                 dma(2, nx // 2 + 1),
+                pltpu.SemaphoreType.REGULAR((2,)),
             ],
             compiler_params=pltpu.CompilerParams(
                 collective_id=0, has_side_effects=True, vmem_limit_bytes=24 * 1024 * 1024

time: 79.8 us -> 76.4 us (0.957)
  Pallas kernels: 79 us -> 75.6 us
    pallas_call x1, Pallas kernels: 74.1 us -> 70.6 us  [on_device(): pl.pallas_call(functools.partial(gather_kernel, ny, nz, nx, rows), out_sh...]
where the time goes in v3:
time: 76.4 us; the launch traced here: 76.2 us
  Pallas kernels  75.6 us (99%)
    pallas_call x1, Pallas kernels, on_device(): pl.pallas_call(functools.partial(gather_kernel, ny, nz, nx, rows), out_sh...  70.6 us
    pallas_call x1, Pallas kernels, on_device(): pl.pallas_call(write_kernel, out_shape=(jax.ShapeDtypeStruct((total_rows,...  4.94 us

profile of v3, /device:TPU:1, one launch (start us, length us, event | category | flops | bytes accessed | tf_op | source)
XLA Modules:
  0.0 76.2 jit_solution(12190000045287718656)
XLA Ops:
  0.6 70.6 %gather.1 = (bf16[16,2816,128]{2,1,0:T(8,128)(2,1)S(1)}, f32[2,1408]{1,0:T(2,128)S(1)}, bf16[64,2048]{1,0:T(8,128)(2,1)S(1)}, f32[2816,128]{1,0:T(8,128)S(1)}) custom-call(f32[2816,128]{1,0:T(8,128)} %bitcast.7, f32[2816,128]{1,0:T(8,128)} %bitcast.8, f32[2,128]{1,0:T(2,128)} %bitcast.9, f32[1,128]{1,0:T(1,128)} %bitcast.10), custom_call_target="tpu_custom_call" | custom-call | tf_op jit(solution)/shard_map/gather/pallas_call | solution.py:469
  71.3 4.9 %write.1 = (bf16[2816,2048]{1,0:T(8,128)(2,1)}, f32[2,1408]{1,0:T(2,128)}, bf16[64,2048]{1,0:T(8,128)(2,1)}, f32[2816,128]{1,0:T(8,128)}) custom-call(bf16[16,2816,128]{2,1,0:T(8,128)(2,1)S(1)} %get-tuple-element.12.land, f32[2,1408]{1,0:T(2,128)S(1)} %get-tuple-element.13.scale_in, bf16[64,2048]{1,0:T(8,128)(2,1)S(1)} %get-tuple-element.14.router_in, ...), custom_call_target="tpu_custom_call" | custom-call | tf_op jit(solution)/shard_map/write/pallas_call | solution.py:522

commit v4 on v3

--- a/solution.py
+++ b/solution.py
@@ -446,8 +446,8 @@
     copies.append(pltpu.make_async_copy(scale_in, scale, sem.at[n]))
     copies.append(pltpu.make_async_copy(router_in, router, sem.at[n + 1]))
     copies.append(pltpu.make_async_copy(latest_in, latest, sem.at[n + 2]))
-    for c in copies:
-        c.start()
+    for i, c in enumerate(copies):
+        c.start(priority=i % 2)
     for c in copies:
         c.wait()
 

time: 76.4 us -> 76.4 us (level)
  no operation moved by 1% of the time
where the time goes in v4:
time: 76.4 us; the launch traced here: 76.2 us
  Pallas kernels  75.5 us (99%)
    pallas_call x1, Pallas kernels, on_device(): pl.pallas_call(functools.partial(gather_kernel, ny, nz, nx, rows), out_sh...  70.6 us
    pallas_call x1, Pallas kernels, on_device(): pl.pallas_call(write_kernel, out_shape=(jax.ShapeDtypeStruct((total_rows,...  4.9 us

profile of v4, /device:TPU:1, one launch (start us, length us, event | category | flops | bytes accessed | tf_op | source)
XLA Modules:
  0.0 76.2 jit_solution(10914119374060935704)
XLA Ops:
  0.6 70.6 %gather.1 = (bf16[16,2816,128]{2,1,0:T(8,128)(2,1)S(1)}, f32[2,1408]{1,0:T(2,128)S(1)}, bf16[64,2048]{1,0:T(8,128)(2,1)S(1)}, f32[2816,128]{1,0:T(8,128)S(1)}) custom-call(f32[2816,128]{1,0:T(8,128)} %bitcast.7, f32[2816,128]{1,0:T(8,128)} %bitcast.8, f32[2,128]{1,0:T(2,128)} %bitcast.9, f32[1,128]{1,0:T(1,128)} %bitcast.10), custom_call_target="tpu_custom_call" | custom-call | tf_op jit(solution)/shard_map/gather/pallas_call | solution.py:469
  71.3 4.9 %write.1 = (bf16[2816,2048]{1,0:T(8,128)(2,1)}, f32[2,1408]{1,0:T(2,128)}, bf16[64,2048]{1,0:T(8,128)(2,1)}, f32[2816,128]{1,0:T(8,128)}) custom-call(bf16[16,2816,128]{2,1,0:T(8,128)(2,1)S(1)} %get-tuple-element.12.land, f32[2,1408]{1,0:T(2,128)S(1)} %get-tuple-element.13.scale_in, bf16[64,2048]{1,0:T(8,128)(2,1)S(1)} %get-tuple-element.14.router_in, ...), custom_call_target="tpu_custom_call" | custom-call | tf_op jit(solution)/shard_map/write/pallas_call | solution.py:522
